TPU v7x, 32 devices: a whole 2x2x4 slice. The times are simulated.
32 devices in a mesh: grp: 8 (over z, y), row: 4 (over x, core).
Axes of the slice: x: 2, y: 2, z: 4, core: 2. Of those that a mesh axis runs over, the one named last changes fastest.
Arguments:
- block: bfloat16 [8192, 1024], P(('grp', 'row')), may hold values from -6 to 6
- degree: int32 [8192], P(('grp', 'row')), may hold values from 1 to 3
- tile_values: bfloat16 [2048, 128, 128], P(('grp', 'row')), may hold values from -0.1875 to 0.1875
- tile_rows: int32 [2048], P(('grp', 'row')), may hold values from 0 to 1
- tile_cols: int32 [2048], P(('grp', 'row')), may hold values from 0 to 15
- tile_count: int32 [32], P(('grp', 'row')), may hold values from 24 to 64, as said below
- send_tiles: int32 [32, 8], P(('grp', 'row')), may hold values from 0 to 1
Outputs:
- logs: bfloat16 [8192, 1024], P(('grp', 'row'))
- gram: float32 [8192, 1024], P(('grp', 'row'))
Inputs may be any that keep to these rules, and one draw needn't show every extreme that they name: Slots of a device at positions tile_count or later are padding; some device has all 64 slots live.
All inputs are finite; a program needn't handle non-finite values.
Results may differ from a plain program's by a relative error of at most 0.014.
Values may be sent and summed in bfloat16 or wider, within the bound.
A program may use at most 128 MiB of HBM per device.

v0:
```python
import jax
import jax.numpy as jnp
from jax import lax
from jax.sharding import PartitionSpec as P

POWERS = 2


def tile_products(sources, tile_values, tile_rows, tile_cols, live_count, row_tiles):
    slots = tile_values.shape[0]
    tile = tile_values.shape[1]
    width = sources.shape[2]
    block_size = 8
    tile_ids = jnp.arange(row_tiles, dtype=jnp.int32)

    def add_block(block_index, totals):
        first_slot = block_index * block_size
        values_block = lax.dynamic_slice_in_dim(tile_values, first_slot, block_size, 0)
        column_ids = lax.dynamic_slice_in_dim(tile_cols, first_slot, block_size, 0)
        row_ids = lax.dynamic_slice_in_dim(tile_rows, first_slot, block_size, 0)
        picked = jnp.take(sources, column_ids, axis=0)
        products = jnp.einsum(
            "sik,skf->sif", values_block, picked, preferred_element_type=jnp.float32
        )
        live_mask = first_slot + jnp.arange(block_size, dtype=jnp.int32) < live_count
        weights = ((row_ids[None, :] == tile_ids[:, None]) & live_mask[None, :]).astype(jnp.float32)
        return totals + jnp.einsum(
            "rs,sif->rif", weights, products, precision=lax.Precision.HIGHEST
        )

    start_totals = jnp.zeros((row_tiles, tile, width), jnp.float32)
    return lax.fori_loop(0, slots // block_size, add_block, start_totals)


def body(block, degree, tile_values, tile_rows, tile_cols, tile_count, send_tiles):
    rows_here, width = block.shape
    tile = tile_values.shape[1]
    row_tiles = rows_here // tile
    ranks = lax.axis_size("row")
    divisor = degree.astype(jnp.float32)[:, None]
    current = block
    power_sum = jnp.zeros(block.shape, jnp.float32)
    for power in range(POWERS):
        gathered = lax.all_gather(current, "row", axis=0, tiled=True)
        own_tiles = current.reshape(row_tiles, tile, width)
        outgoing = jnp.take(own_tiles, send_tiles[0], axis=0)
        incoming = lax.all_to_all(outgoing, "grp", split_axis=0, concat_axis=0, tiled=True)
        sources = jnp.concatenate([gathered.reshape(-1, tile, width), incoming], axis=0)
        summed = tile_products(sources, tile_values, tile_rows, tile_cols, tile_count[0], row_tiles)
        current = (summed.reshape(rows_here, width) / divisor).astype(jnp.bfloat16)
        power_sum = power_sum + current.astype(jnp.float32)
    logs = jnp.log(jnp.maximum(3.0 * power_sum, 1.0)).astype(jnp.bfloat16)
    share = width // ranks
    contract = (((0,), (0,)), ((), ()))
    everyone = lax.all_gather(logs, "row", axis=0, tiled=True)
    columns = lax.dynamic_slice_in_dim(everyone, lax.axis_index("row") * share, share, 1)
    gram = lax.dot_general(columns, everyone, contract, preferred_element_type=jnp.float32)
    return (logs, gram / (rows_here * ranks))


def solution(mesh):
    placed = (
        P(("grp", "row"), None),
        P(("grp", "row")),
        P(("grp", "row"), None, None),
        P(("grp", "row")),
        P(("grp", "row")),
        P(("grp", "row")),
        P(("grp", "row"), None),
    )
    return jax.shard_map(
        body,
        mesh=mesh,
        in_specs=placed,
        out_specs=(P(("grp", "row"), None), P(("grp", "row"), None)),
        check_vma=False,
    )
```

profile of v0, /device:TPU:13, one launch (start us, length us, event | category | flops | bytes accessed | tf_op | source)
XLA Modules:
  0.0 401.2 jit_solution(6377621890501378388)
XLA Ops:
  11.8 5.8 %all-to-all-start = ((bf16[8,128,1024]{2,1,0:T(8,128)(2,1)}), bf16[8,128,1024]{2,1,0:T(8,128)(2,1)S(1)}, u32[]{:S(2)}, u32[]{:S(2)}) async-start(bf16[8,128,1024]{2,1,0:T(8,128)(2,1)} %broadcast_select_fusion.1), calls=%async_computation | async-start | bytes 4194304 | tf_op jit(solution)/shard_map/all_to_all | solution.py:47
  18.4 26.0 %all-gather.4.cloned.1.call-done = bf16[1024,1024]{1,0:T(8,128)(2,1)} async-done(((bf16[256,1024]{1,0:T(8,128)(2,1)}), bf16[1024,1024]{1,0:T(8,128)(2,1)}) %all-gather.4.cloned.1.call-update) | async-done | bytes 2097168 | tf_op jit(solution)/shard_map/all_gather | solution.py:44
  44.4 18.9 %all-to-all-done = bf16[8,128,1024]{2,1,0:T(8,128)(2,1)S(1)} async-done(((bf16[8,128,1024]{2,1,0:T(8,128)(2,1)}), bf16[8,128,1024]{2,1,0:T(8,128)(2,1)S(1)}, u32[]{:S(2)}, u32[]{:S(2)}) %all-to-all-start) | async-done | bytes 2097184 | tf_op jit(solution)/shard_map/all_to_all | solution.py:47
  63.3 3.9 pad_maximum_fusion
  67.2 117.3 %while.28 = (s32[]{:T(128)}, f32[2,128,1024]{2,0,1:T(2,128)S(1)}, s32[64]{0:T(128)S(1)}, s32[]{:T(128)}, bf16[64,128,128]{2,1,0:T(8,128)(2,1)}, /*index=5*/s32[6...) while((s32[]{:T(128)}, f32[2,128,1024]{2,0,1:T(2,128)S(1)}, ...), condition=%wide.region_1.4_spmd.clone, body=%wide.region_0.3_spmd.clone.sunk | while | flops 295175264 | bytes 17043896 | solution.py:32
  70.9 3.7 fusion.61
  74.7 7.2 %fusion.62 = f32[2,128,1024]{2,0,1:T(2,128)S(1)} fusion(f32[8,128,1024]{2,1,0:T(8,128)} %fusion.61, f32[2,128,1024]{2,0,1:T(2,128)S(1)} %get-tuple-element.484, pred[]{:T(512)S(6)} %compare.6, pred[8]{0:T(512)(128)(4,1)S(1)} %get-tuple-element.461, s32[8]{0:T(128)S(1)} %dynamic_slice.67), kind=kOutput, calls=%fused_computation.11.clone.1 | convolution fusion | flops 25690144 | bytes 6291497 | tf_op jit(solution)/shard_map/while/body/eval_jaxpr/rs,sif->rif/dot_general | solution.py:27
  85.5 3.7 fusion.61
  89.3 7.2 %fusion.62 = f32[2,128,1024]{2,0,1:T(2,128)S(1)} fusion(f32[8,128,1024]{2,1,0:T(8,128)} %fusion.61, f32[2,128,1024]{2,0,1:T(2,128)S(1)} %get-tuple-element.484, pred[]{:T(512)S(6)} %compare.6, pred[8]{0:T(512)(128)(4,1)S(1)} %get-tuple-element.461, s32[8]{0:T(128)S(1)} %dynamic_slice.67), kind=kOutput, calls=%fused_computation.11.clone.1 | convolution fusion | flops 25690144 | bytes 6291497 | tf_op jit(solution)/shard_map/while/body/eval_jaxpr/rs,sif->rif/dot_general | solution.py:27
  100.2 3.7 fusion.61
  104.0 7.2 %fusion.62 = f32[2,128,1024]{2,0,1:T(2,128)S(1)} fusion(f32[8,128,1024]{2,1,0:T(8,128)} %fusion.61, f32[2,128,1024]{2,0,1:T(2,128)S(1)} %get-tuple-element.484, pred[]{:T(512)S(6)} %compare.6, pred[8]{0:T(512)(128)(4,1)S(1)} %get-tuple-element.461, s32[8]{0:T(128)S(1)} %dynamic_slice.67), kind=kOutput, calls=%fused_computation.11.clone.1 | convolution fusion | flops 25690144 | bytes 6291497 | tf_op jit(solution)/shard_map/while/body/eval_jaxpr/rs,sif->rif/dot_general | solution.py:27
  112.0 2.9 gather_fusion
  114.8 3.7 fusion.61
  118.6 7.2 %fusion.62 = f32[2,128,1024]{2,0,1:T(2,128)S(1)} fusion(f32[8,128,1024]{2,1,0:T(8,128)} %fusion.61, f32[2,128,1024]{2,0,1:T(2,128)S(1)} %get-tuple-element.484, pred[]{:T(512)S(6)} %compare.6, pred[8]{0:T(512)(128)(4,1)S(1)} %get-tuple-element.461, s32[8]{0:T(128)S(1)} %dynamic_slice.67), kind=kOutput, calls=%fused_computation.11.clone.1 | convolution fusion | flops 25690144 | bytes 6291497 | tf_op jit(solution)/shard_map/while/body/eval_jaxpr/rs,sif->rif/dot_general | solution.py:27
  126.6 2.9 gather_fusion
  129.5 3.7 fusion.61
  133.3 7.2 %fusion.62 = f32[2,128,1024]{2,0,1:T(2,128)S(1)} fusion(f32[8,128,1024]{2,1,0:T(8,128)} %fusion.61, f32[2,128,1024]{2,0,1:T(2,128)S(1)} %get-tuple-element.484, pred[]{:T(512)S(6)} %compare.6, pred[8]{0:T(512)(128)(4,1)S(1)} %get-tuple-element.461, s32[8]{0:T(128)S(1)} %dynamic_slice.67), kind=kOutput, calls=%fused_computation.11.clone.1 | convolution fusion | flops 25690144 | bytes 6291497 | tf_op jit(solution)/shard_map/while/body/eval_jaxpr/rs,sif->rif/dot_general | solution.py:27
  144.2 3.7 fusion.61
  148.0 7.2 %fusion.62 = f32[2,128,1024]{2,0,1:T(2,128)S(1)} fusion(f32[8,128,1024]{2,1,0:T(8,128)} %fusion.61, f32[2,128,1024]{2,0,1:T(2,128)S(1)} %get-tuple-element.484, pred[]{:T(512)S(6)} %compare.6, pred[8]{0:T(512)(128)(4,1)S(1)} %get-tuple-element.461, s32[8]{0:T(128)S(1)} %dynamic_slice.67), kind=kOutput, calls=%fused_computation.11.clone.1 | convolution fusion | flops 25690144 | bytes 6291497 | tf_op jit(solution)/shard_map/while/body/eval_jaxpr/rs,sif->rif/dot_general | solution.py:27
  155.9 2.9 gather_fusion
  158.8 3.7 fusion.61
  162.6 7.2 %fusion.62 = f32[2,128,1024]{2,0,1:T(2,128)S(1)} fusion(f32[8,128,1024]{2,1,0:T(8,128)} %fusion.61, f32[2,128,1024]{2,0,1:T(2,128)S(1)} %get-tuple-element.484, pred[]{:T(512)S(6)} %compare.6, pred[8]{0:T(512)(128)(4,1)S(1)} %get-tuple-element.461, s32[8]{0:T(128)S(1)} %dynamic_slice.67), kind=kOutput, calls=%fused_computation.11.clone.1 | convolution fusion | flops 25690144 | bytes 6291497 | tf_op jit(solution)/shard_map/while/body/eval_jaxpr/rs,sif->rif/dot_general | solution.py:27
  173.5 3.7 fusion.61
  177.3 7.2 %fusion.62 = f32[2,128,1024]{2,0,1:T(2,128)S(1)} fusion(f32[8,128,1024]{2,1,0:T(8,128)} %fusion.61, f32[2,128,1024]{2,0,1:T(2,128)S(1)} %get-tuple-element.484, pred[]{:T(512)S(6)} %compare.6, pred[8]{0:T(512)(128)(4,1)S(1)} %get-tuple-element.461, s32[8]{0:T(128)S(1)} %dynamic_slice.67), kind=kOutput, calls=%fused_computation.11.clone.1 | convolution fusion | flops 25690144 | bytes 6291497 | tf_op jit(solution)/shard_map/while/body/eval_jaxpr/rs,sif->rif/dot_general | solution.py:27
  186.9 3.2 broadcast_select_fusion
  190.1 6.3 %all-to-all-start.1 = ((bf16[8,128,1024]{2,1,0:T(8,128)(2,1)}), bf16[8,128,1024]{2,1,0:T(8,128)(2,1)}, u32[]{:S(2)}, u32[]{:S(2)}) async-start(bf16[8,128,1024]{2,1,0:T(8,128)(2,1)} %broadcast_select_fusion), calls=%async_computation.1 | async-start | bytes 4194304 | tf_op jit(solution)/shard_map/all_to_all | solution.py:47
  197.6 26.6 %all-gather.6.cloned.1.call-done = bf16[1024,1024]{1,0:T(8,128)(2,1)} async-done(((bf16[256,1024]{1,0:T(8,128)(2,1)}), bf16[1024,1024]{1,0:T(8,128)(2,1)}) %all-gather.6.cloned.1.call-update) | async-done | bytes 2097168 | tf_op jit(solution)/shard_map/all_gather | solution.py:44
  224.2 17.9 %all-to-all-done.1 = bf16[8,128,1024]{2,1,0:T(8,128)(2,1)} async-done(((bf16[8,128,1024]{2,1,0:T(8,128)(2,1)}), bf16[8,128,1024]{2,1,0:T(8,128)(2,1)}, u32[]{:S(2)}, u32[]{:S(2)}) %all-to-all-start.1) | async-done | bytes 2097184 | tf_op jit(solution)/shard_map/all_to_all | solution.py:47
  242.1 4.5 %pad_maximum_fusion.1 = bf16[16,128,1024]{2,1,0:T(8,128)(2,1)} fusion(bf16[8,128,1024]{2,1,0:T(8,128)(2,1)} %all-to-all-done.1, bf16[8,128,1024]{2,1,0:T(8,128)(2,1)} %bitcast.35), kind=kLoop, calls=%fused_computation.47 | loop fusion | flops 2097152 | bytes 8388608 | tf_op jit(solution)/shard_map/concatenate | solution.py:48
  246.7 117.3 %while.29 = (s32[]{:T(128)}, f32[2,128,1024]{2,0,1:T(2,128)S(1)}, s32[64]{0:T(128)S(1)}, s32[]{:T(128)}, bf16[64,128,128]{2,1,0:T(8,128)(2,1)}, /*index=5*/s32[6...) while((s32[]{:T(128)}, f32[2,128,1024]{2,0,1:T(2,128)S(1)}, ...), condition=%wide.region_3.6_spmd.clone, body=%wide.region_2.5_spmd.clone.sunk | while | flops 295175264 | bytes 17043896 | solution.py:32
  250.3 3.7 fusion.67
  254.1 7.2 %fusion.68 = f32[2,128,1024]{2,0,1:T(2,128)S(1)} fusion(f32[8,128,1024]{2,1,0:T(8,128)} %fusion.67, f32[2,128,1024]{2,0,1:T(2,128)S(1)} %get-tuple-element.517, pred[]{:T(512)S(6)} %compare.7, pred[8]{0:T(512)(128)(4,1)S(1)} %get-tuple-element.471, s32[8]{0:T(128)S(1)} %dynamic_slice.69), kind=kOutput, calls=%fused_computation.31.clone.1 | convolution fusion | flops 25690144 | bytes 6291497 | tf_op jit(solution)/shard_map/while/body/eval_jaxpr/rs,sif->rif/dot_general | solution.py:27
  264.9 3.7 fusion.67
  268.7 7.2 %fusion.68 = f32[2,128,1024]{2,0,1:T(2,128)S(1)} fusion(f32[8,128,1024]{2,1,0:T(8,128)} %fusion.67, f32[2,128,1024]{2,0,1:T(2,128)S(1)} %get-tuple-element.517, pred[]{:T(512)S(6)} %compare.7, pred[8]{0:T(512)(128)(4,1)S(1)} %get-tuple-element.471, s32[8]{0:T(128)S(1)} %dynamic_slice.69), kind=kOutput, calls=%fused_computation.31.clone.1 | convolution fusion | flops 25690144 | bytes 6291497 | tf_op jit(solution)/shard_map/while/body/eval_jaxpr/rs,sif->rif/dot_general | solution.py:27
  279.6 3.7 fusion.67
  283.4 7.2 %fusion.68 = f32[2,128,1024]{2,0,1:T(2,128)S(1)} fusion(f32[8,128,1024]{2,1,0:T(8,128)} %fusion.67, f32[2,128,1024]{2,0,1:T(2,128)S(1)} %get-tuple-element.517, pred[]{:T(512)S(6)} %compare.7, pred[8]{0:T(512)(128)(4,1)S(1)} %get-tuple-element.471, s32[8]{0:T(128)S(1)} %dynamic_slice.69), kind=kOutput, calls=%fused_computation.31.clone.1 | convolution fusion | flops 25690144 | bytes 6291497 | tf_op jit(solution)/shard_map/while/body/eval_jaxpr/rs,sif->rif/dot_general | solution.py:27
  294.2 3.7 fusion.67
  298.1 7.2 %fusion.68 = f32[2,128,1024]{2,0,1:T(2,128)S(1)} fusion(f32[8,128,1024]{2,1,0:T(8,128)} %fusion.67, f32[2,128,1024]{2,0,1:T(2,128)S(1)} %get-tuple-element.517, pred[]{:T(512)S(6)} %compare.7, pred[8]{0:T(512)(128)(4,1)S(1)} %get-tuple-element.471, s32[8]{0:T(128)S(1)} %dynamic_slice.69), kind=kOutput, calls=%fused_computation.31.clone.1 | convolution fusion | flops 25690144 | bytes 6291497 | tf_op jit(solution)/shard_map/while/body/eval_jaxpr/rs,sif->rif/dot_general | solution.py:27
  308.9 3.7 fusion.67
  312.7 7.2 %fusion.68 = f32[2,128,1024]{2,0,1:T(2,128)S(1)} fusion(f32[8,128,1024]{2,1,0:T(8,128)} %fusion.67, f32[2,128,1024]{2,0,1:T(2,128)S(1)} %get-tuple-element.517, pred[]{:T(512)S(6)} %compare.7, pred[8]{0:T(512)(128)(4,1)S(1)} %get-tuple-element.471, s32[8]{0:T(128)S(1)} %dynamic_slice.69), kind=kOutput, calls=%fused_computation.31.clone.1 | convolution fusion | flops 25690144 | bytes 6291497 | tf_op jit(solution)/shard_map/while/body/eval_jaxpr/rs,sif->rif/dot_general | solution.py:27
  323.6 3.7 fusion.67
  327.4 7.2 %fusion.68 = f32[2,128,1024]{2,0,1:T(2,128)S(1)} fusion(f32[8,128,1024]{2,1,0:T(8,128)} %fusion.67, f32[2,128,1024]{2,0,1:T(2,128)S(1)} %get-tuple-element.517, pred[]{:T(512)S(6)} %compare.7, pred[8]{0:T(512)(128)(4,1)S(1)} %get-tuple-element.471, s32[8]{0:T(128)S(1)} %dynamic_slice.69), kind=kOutput, calls=%fused_computation.31.clone.1 | convolution fusion | flops 25690144 | bytes 6291497 | tf_op jit(solution)/shard_map/while/body/eval_jaxpr/rs,sif->rif/dot_general | solution.py:27
  338.2 3.7 fusion.67
  342.0 7.2 %fusion.68 = f32[2,128,1024]{2,0,1:T(2,128)S(1)} fusion(f32[8,128,1024]{2,1,0:T(8,128)} %fusion.67, f32[2,128,1024]{2,0,1:T(2,128)S(1)} %get-tuple-element.517, pred[]{:T(512)S(6)} %compare.7, pred[8]{0:T(512)(128)(4,1)S(1)} %get-tuple-element.471, s32[8]{0:T(128)S(1)} %dynamic_slice.69), kind=kOutput, calls=%fused_computation.31.clone.1 | convolution fusion | flops 25690144 | bytes 6291497 | tf_op jit(solution)/shard_map/while/body/eval_jaxpr/rs,sif->rif/dot_general | solution.py:27
  352.9 3.7 fusion.67
  356.7 7.2 %fusion.68 = f32[2,128,1024]{2,0,1:T(2,128)S(1)} fusion(f32[8,128,1024]{2,1,0:T(8,128)} %fusion.67, f32[2,128,1024]{2,0,1:T(2,128)S(1)} %get-tuple-element.517, pred[]{:T(512)S(6)} %compare.7, pred[8]{0:T(512)(128)(4,1)S(1)} %get-tuple-element.471, s32[8]{0:T(128)S(1)} %dynamic_slice.69), kind=kOutput, calls=%fused_computation.31.clone.1 | convolution fusion | flops 25690144 | bytes 6291497 | tf_op jit(solution)/shard_map/while/body/eval_jaxpr/rs,sif->rif/dot_general | solution.py:27
  366.3 24.8 %all-gather.8.cloned.1.call-done = bf16[1024,1024]{1,0:T(8,128)(2,1)} async-done(((bf16[256,1024]{1,0:T(8,128)(2,1)}), bf16[1024,1024]{1,0:T(8,128)(2,1)}) %all-gather.8.cloned.1.call-update) | async-done | bytes 2097168 | tf_op jit(solution)/shard_map/all_gather | solution.py:55
  391.2 3.5 convolution_multiply_fusion
  (90 shorter events, 61.5 us)
Async XLA Ops:
  11.8 6.5 %copy-start.3 = (s32[256]{0:T(256)S(1)}, s32[256]{0:T(256)}, u32[]{:S(2)}) copy-start(s32[256]{0:T(256)} %param.16) | copy-start | bytes 3076
  11.8 51.5 %all-to-all-start = ((bf16[8,128,1024]{2,1,0:T(8,128)(2,1)}), bf16[8,128,1024]{2,1,0:T(8,128)(2,1)S(1)}, u32[]{:S(2)}, u32[]{:S(2)}) async-start(bf16[8,128,1024]{2,1,0:T(8,128)(2,1)} %broadcast_select_fusion.1), calls=%async_computation | async-start | bytes 4194304 | tf_op jit(solution)/shard_map/all_to_all | solution.py:47
  17.6 26.8 %all-gather.4.cloned.1.call-start = ((), (), s32[]{:S(2)}) async-start(), calls=%async_computation.2 | async-start | bytes 2621440 | tf_op jit(solution)/shard_map/all_gather | solution.py:44
  63.3 3.9 copy-start.2
  63.3 3.9 copy-start.4
  184.9 11.5 %copy-start = (f32[2,128,1024]{2,1,0:T(8,128)}, f32[2,128,1024]{2,1,0:T(8,128)S(1)}, u32[]{:S(2)}) copy-start(f32[2,128,1024]{2,1,0:T(8,128)S(1)} %get-tuple-element.371) | copy-start | bytes 3145732
  190.1 52.1 %all-to-all-start.1 = ((bf16[8,128,1024]{2,1,0:T(8,128)(2,1)}), bf16[8,128,1024]{2,1,0:T(8,128)(2,1)}, u32[]{:S(2)}, u32[]{:S(2)}) async-start(bf16[8,128,1024]{2,1,0:T(8,128)(2,1)} %broadcast_select_fusion), calls=%async_computation.1 | async-start | bytes 4194304 | tf_op jit(solution)/shard_map/all_to_all | solution.py:47
  196.4 27.8 %all-gather.6.cloned.1.call-start = ((), (), s32[]{:S(2)}) async-start(), calls=%async_computation.3 | async-start | bytes 2621440 | tf_op jit(solution)/shard_map/all_gather | solution.py:44
  197.4 193.8 %all-gather.8.cloned.1.call-start = ((), (), s32[]{:S(2)}) async-start(), calls=%async_computation.4 | async-start | bytes 2621440 | tf_op jit(solution)/shard_map/all_gather | solution.py:55
  363.9 1.2 copy-start.1
Sparse Core Ops, SparseCore 0:
  20.0 24.3 all-gather.3
  199.4 24.8 all-gather.5
  366.5 24.6 all-gather.7
where the time goes:
time: 405 us; the launch traced here: 401 us
  matrix products  179 us (44%)
  waiting for transfers between devices  115 us (28%)
  local copies, waits for them, and re-layouts  52 us (13%)
  other arithmetic  28.7 us (7%)
  between operations  13.8 us (3%)
  starting transfers between devices  12.4 us (3%)
    dot_general x16, matrix products, add_block(): jnp.einsum('rs,sif->rif', weights, products, precision=lax.Precision.HIGH...  116 us
    dot_general x16, matrix products, add_block(): jnp.einsum('sik,skf->sif', values_block, picked, preferred_element_type=j...  59.6 us
    all_gather x2, waiting for transfers between devices, body(): gathered = lax.all_gather(current, 'row', axis=0, tiled=True)  52.6 us
    gather x16, local copies, waits for them, and re-layouts, add_block(): picked = jnp.take(sources, column_ids, axis=0)  45.9 us
    all_to_all x2, waiting for transfers between devices, body(): lax.all_to_all(outgoing, 'grp', split_axis=0, concat_axis=0, tiled=True)  36.8 us
    all_gather x1, waiting for transfers between devices, body(): everyone = lax.all_gather(logs, 'row', axis=0, tiled=True)  24.8 us
    all_to_all x2, starting transfers between devices, body(): lax.all_to_all(outgoing, 'grp', split_axis=0, concat_axis=0, tiled=True)  12.1 us
    and x16, other arithmetic, add_block(): picked = jnp.take(sources, column_ids, axis=0)  11.6 us
  transfers between devices with their start and end apart: 5, of which 5 were waited for; matrix products, arithmetic and copies ran while one was open for 0% of the time, Pallas kernels for 0%

commit v1 on v0

v1 whole, which is shorter than its diff:
```python
import functools

import jax
import jax.numpy as jnp
from jax import lax
from jax.experimental import pallas as pl
from jax.experimental.pallas import tpu as pltpu
from jax.sharding import PartitionSpec as P

POWERS = 2
MESH = pl.DeviceIdType.MESH


def matrix_kernel(sources, rows_ref, cols_ref, count_ref, degree_ref, values_ref, out_ref, sums):
    tile = values_ref.shape[1]
    row_tiles = out_ref.shape[0] // tile

    def clear(index, carry):
        sums[index] = jnp.zeros(sums.shape[1:], jnp.float32)
        return carry

    lax.fori_loop(0, row_tiles * sources, clear, 0)

    def add_slot(slot, carry):
        place = rows_ref[slot] * sources + cols_ref[slot]
        sums[place] += values_ref[slot].astype(jnp.float32)
        return carry

    lax.fori_loop(0, count_ref[0], add_slot, 0)
    for row in range(row_tiles):
        degree = degree_ref[row : row + 1, :].astype(jnp.float32)
        scale = (1.0 / jnp.broadcast_to(degree, (tile, tile))).T
        for col in range(sources):
            part = sums[row * sources + col] * scale
            out_ref[row * tile : (row + 1) * tile, col * tile : (col + 1) * tile] = part.astype(jnp.bfloat16)


def step_kernel(
    groups, ranks, send_ref, matrix_ref, block_ref, logs_ref, gram_ref,
    source, own, staged, total, everyone, mine,
    grp_send, grp_recv, row_send, row_recv, pass_send,
):
    chunks, _, row_tiles, tile, width = own.shape
    local = ranks * row_tiles
    g = lax.axis_index("grp")
    r = lax.axis_index("row")
    core = lax.rem(r, 2)
    partner = r + 1 - 2 * core
    pairs = ranks // 2

    def other_group(step):
        return lax.rem(g + step, groups)

    def same_core(step):
        return lax.rem(r + 2 * step, ranks)

    barrier = pltpu.get_barrier_semaphore()
    for step in range(1, groups):
        pl.semaphore_signal(barrier, inc=1, device_id=(other_group(step), r), device_id_type=MESH)
    for step in range(1, ranks):
        pl.semaphore_signal(barrier, inc=1, device_id=(g, lax.rem(r + step, ranks)), device_id_type=MESH)

    def land(phase, j, rank):
        where = pl.ds(rank * row_tiles, row_tiles)
        return source.at[phase, j, where] if phase < POWERS else everyone.at[j, where]

    def row_copy(phase, j, to):
        origin = own.at[j, phase]
        return pltpu.make_async_remote_copy(
            src_ref=origin, dst_ref=land(phase, j, r),
            send_sem=row_send.at[phase, j, to], recv_sem=row_recv.at[phase, j, r],
            device_id=(g, to), device_id_type=MESH)

    def pass_copy(phase, j, rank):
        spot = land(phase, j, rank)
        return pltpu.make_async_remote_copy(
            src_ref=spot, dst_ref=spot,
            send_sem=pass_send.at[phase, j, rank], recv_sem=row_recv.at[phase, j, rank],
            device_id=(g, partner), device_id_type=MESH)

    def row_arrival(phase, j, rank):
        spot = land(phase, j, rank)
        return pltpu.make_async_remote_copy(
            src_ref=spot, dst_ref=spot,
            send_sem=pass_send.at[phase, j, rank], recv_sem=row_recv.at[phase, j, rank],
            device_id=(g, partner), device_id_type=MESH)

    def grp_copy(phase, j, to):
        return pltpu.make_async_remote_copy(
            src_ref=staged.at[phase, j, to], dst_ref=source.at[phase, j, local + g],
            send_sem=grp_send.at[phase, j, to], recv_sem=grp_recv.at[phase, j, g],
            device_id=(to, r), device_id_type=MESH)

    def grp_arrival(phase, j, group):
        return pltpu.make_async_remote_copy(
            src_ref=staged.at[phase, j, group], dst_ref=source.at[phase, j, local + group],
            send_sem=grp_send.at[phase, j, group], recv_sem=grp_recv.at[phase, j, group],
            device_id=(group, r), device_id_type=MESH)

    def stage(phase, j):
        for step in range(1, groups):
            to = other_group(step)
            staged[phase, j, to] = own[j, phase, send_ref[0, to]]
        source[phase, j, local + g] = own[j, phase, send_ref[0, g]]

    def keep(phase, j, value):
        tiles = value.reshape(row_tiles, tile, width)
        own[j, phase] = tiles
        if phase < POWERS:
            source[phase, j, pl.ds(r * row_tiles, row_tiles)] = tiles
        else:
            everyone[j, pl.ds(r * row_tiles, row_tiles)] = tiles

    def send(phase, j):
        if phase < POWERS:
            for step in range(1, groups):
                grp_copy(phase, j, other_group(step)).start()
        for step in range(1, pairs):
            row_copy(phase, j, same_core(step)).start()
        row_copy(phase, j, partner).start()

    def receive(phase, j):
        for step in range(1, pairs):
            rank = lax.rem(r + ranks - 2 * step, ranks)
            row_arrival(phase, j, rank).wait_recv()
            pass_copy(phase, j, rank).start()
        row_arrival(phase, j, partner).wait_recv()
        for step in range(1, pairs):
            row_arrival(phase, j, lax.rem(partner + ranks - 2 * step, ranks)).wait_recv()
        if phase < POWERS:
            for step in range(1, groups):
                grp_arrival(phase, j, lax.rem(g + groups - step, groups)).wait_recv()

    for j in range(chunks):
        keep(0, j, block_ref[:, j * width : (j + 1) * width])
        stage(0, j)
    pl.semaphore_wait(barrier, groups + ranks - 2)
    for j in range(chunks):
        send(0, j)
    for phase in range(POWERS):
        for j in range(chunks):
            receive(phase, j)
            summed = jnp.dot(
                matrix_ref[...], source[phase, j].reshape(-1, width),
                preferred_element_type=jnp.float32)
            current = summed.astype(jnp.bfloat16)
            if phase == 0:
                total[j] = current.astype(jnp.float32)
            else:
                total[j] += current.astype(jnp.float32)
            if phase < POWERS - 1:
                keep(phase + 1, j, current)
                stage(phase + 1, j)
            else:
                logs = jnp.log(jnp.maximum(3.0 * total[j], 1.0)).astype(jnp.bfloat16)
                logs_ref[:, j * width : (j + 1) * width] = logs
                keep(phase + 1, j, logs)
            send(phase + 1, j)
    for j in range(chunks):
        receive(POWERS, j)
    mine[...] = everyone[r].reshape(-1, width).T
    rows_all = row_tiles * tile * ranks
    for j in range(chunks):
        part = jnp.dot(mine[...], everyone[j].reshape(-1, width), preferred_element_type=jnp.float32)
        gram_ref[:, j * width : (j + 1) * width] = part / rows_all
    for phase in range(POWERS + 1):
        for j in range(chunks):
            if phase < POWERS:
                for step in range(1, groups):
                    grp_copy(phase, j, other_group(step)).wait_send()
            for step in range(1, pairs):
                row_copy(phase, j, same_core(step)).wait_send()
                pass_copy(phase, j, lax.rem(r + ranks - 2 * step, ranks)).wait_send()
            row_copy(phase, j, partner).wait_send()


def body(block, degree, tile_values, tile_rows, tile_cols, tile_count, send_tiles):
    rows_here, width = block.shape
    tile = tile_values.shape[1]
    row_tiles = rows_here // tile
    ranks = lax.axis_size("row")
    groups = lax.axis_size("grp")
    sources = ranks * row_tiles + groups
    smem = pl.BlockSpec(memory_space=pltpu.SMEM)
    vmem = pl.BlockSpec(memory_space=pltpu.VMEM)
    matrix = pl.pallas_call(
        functools.partial(matrix_kernel, sources),
        out_shape=jax.ShapeDtypeStruct((rows_here, sources * tile), jnp.bfloat16),
        in_specs=[smem, smem, smem, vmem, vmem],
        out_specs=vmem,
        scratch_shapes=[pltpu.VMEM((row_tiles * sources, tile, tile), jnp.float32)],
        name="matrix",
    )(tile_rows, tile_cols, tile_count, degree.reshape(row_tiles, tile), tile_values)
    share = width // ranks
    chunks = ranks
    dma = pltpu.SemaphoreType.DMA
    logs, gram = pl.pallas_call(
        functools.partial(step_kernel, groups, ranks),
        out_shape=(
            jax.ShapeDtypeStruct((rows_here, width), jnp.bfloat16),
            jax.ShapeDtypeStruct((share, width), jnp.float32),
        ),
        in_specs=[smem, vmem, vmem],
        out_specs=(vmem, vmem),
        scratch_shapes=[
            pltpu.VMEM((POWERS, chunks, sources, tile, share), jnp.bfloat16),
            pltpu.VMEM((chunks, POWERS + 1, row_tiles, tile, share), jnp.bfloat16),
            pltpu.VMEM((POWERS, chunks, groups, tile, share), jnp.bfloat16),
            pltpu.VMEM((chunks, rows_here, share), jnp.float32),
            pltpu.VMEM((chunks, ranks * row_tiles, tile, share), jnp.bfloat16),
            pltpu.VMEM((share, rows_here * ranks), jnp.bfloat16),
            dma((POWERS, chunks, groups)),
            dma((POWERS, chunks, groups)),
            dma((POWERS + 1, chunks, ranks)),
            dma((POWERS + 1, chunks, ranks)),
            dma((POWERS + 1, chunks, ranks)),
        ],
        compiler_params=pltpu.CompilerParams(
            collective_id=0, has_side_effects=True, vmem_limit_bytes=60 * 1024 * 1024),
        name="step",
    )(send_tiles, matrix, block)
    return logs, gram


def solution(mesh):
    placed = (
        P(("grp", "row"), None),
        P(("grp", "row")),
        P(("grp", "row"), None, None),
        P(("grp", "row")),
        P(("grp", "row")),
        P(("grp", "row")),
        P(("grp", "row"), None),
    )
    return jax.shard_map(
        body,
        mesh=mesh,
        in_specs=placed,
        out_specs=(P(("grp", "row"), None), P(("grp", "row"), None)),
        check_vma=False,
    )
```

time: 405 us -> 117 us (0.29)
  matrix products: 179 us -> 0 us
  waiting for transfers between devices: 115 us -> 0 us
  Pallas kernels: 0 us -> 111 us
  local copies, waits for them, and re-layouts: 52 us -> 4.17 us
  other arithmetic: 28.7 us -> 0 us
  between operations: 13.8 us -> 1.29 us
  starting transfers between devices: 12.4 us -> 0 us
    dot_general x33 -> x0, matrix products: 179 us -> none  [the longest x16 116 us: add_block(): jnp.einsum('rs,sif->rif', weights, products, precision=lax.Precision.HIGH...]
    pallas_call x0 -> x2, Pallas kernels: none -> 111 us  [the longest x1 108 us: body(): pl.pallas_call(functools.partial(step_kernel, groups, ranks), out_shape=(...]
    all_gather x3 -> x0, waiting for transfers between devices: 77.5 us -> none  [the longest x2 52.6 us: body(): gathered = lax.all_gather(current, 'row', axis=0, tiled=True)]
    gather x18 -> x0, local copies, waits for them, and re-layouts: 49.6 us -> none  [the longest x16 45.9 us: add_block(): picked = jnp.take(sources, column_ids, axis=0)]
    all_to_all x2 -> x0, waiting for transfers between devices: 36.8 us -> none  [body(): lax.all_to_all(outgoing, 'grp', split_axis=0, concat_axis=0, tiled=True)]
    and x17 -> x0, other arithmetic: 12.3 us -> none  [the longest x16 11.6 us: add_block(): picked = jnp.take(sources, column_ids, axis=0)]
    all_to_all x2 -> x0, starting transfers between devices: 12.1 us -> none  [body(): lax.all_to_all(outgoing, 'grp', split_axis=0, concat_axis=0, tiled=True)]
    concatenate x2 -> x0, other arithmetic: 8.43 us -> none  [body(): jnp.concatenate([gathered.reshape(-1, tile, width), incoming], axis=0)]
  transfers between devices with their start and end apart: 5 -> 0, of which waited for: 5 -> 0; matrix products, arithmetic and copies ran while one was open for 0% -> 0% of each run, Pallas kernels for 0% -> 0%
where the time goes in v1:
time: 117 us
  Pallas kernels  111 us (95%)
  local copies, waits for them, and re-layouts  4.17 us (4%)
  between operations  1.29 us (1%)
    pallas_call x1, Pallas kernels, body(): pl.pallas_call(functools.partial(step_kernel, groups, ranks), out_shape=(...  108 us
    unnamed x2, local copies, waits for them, and re-layouts  4.17 us
    pallas_call x1, Pallas kernels, body(): pl.pallas_call(functools.partial(matrix_kernel, sources), out_shape=jax.S...  3.73 us

profile of v1, /device:TPU:13, one launch (start us, length us, event | category | flops | bytes accessed | tf_op | source)
XLA Modules:
  0.0 116.8 jit_solution(17397982122808833447)
XLA Ops:
  1.3 3.7 %matrix.1.matrix_ref = bf16[256,2048]{1,0:T(8,128)(2,1)} custom-call(s32[64]{0:T(128)} %rows_ref.1, s32[64]{0:T(128)} %cols_ref.1, s32[1]{0:T(128)S(6)} %copy.11.count_ref, s32[2,128]{1,0:T(2,128)} %bitcast.1, bf16[64,128,128]{2,1,0:T(8,128)(2,1)} %values_ref.1), custom_call_target="tpu_custom_call" | custom-call | tf_op jit(solution)/shard_map/matrix/pallas_call | solution.py:186
  5.0 107.6 %step.1 = (bf16[256,1024]{1,0:T(8,128)(2,1)}, f32[256,1024]{1,0:T(8,128)}) custom-call(s32[1,8]{1,0:T(1,128)} %send_ref.1, bf16[256,2048]{1,0:T(8,128)(2,1)} %matrix.1.matrix_ref, bf16[256,1024]{1,0:T(8,128)(2,1)} %block_ref.1), custom_call_target="tpu_custom_call" | custom-call | tf_op jit(solution)/shard_map/step/pallas_call | solution.py:197
  112.6 1.9 %copy.12 = bf16[256,1024]{1,0:T(8,128)(2,1)} copy(bf16[256,1024]{1,0:T(8,128)(2,1)} %get-tuple-element.4) | data formatting | bytes 1048576
  114.5 2.3 %copy.13 = f32[256,1024]{1,0:T(8,128)} copy(f32[256,1024]{1,0:T(8,128)} %get-tuple-element.5) | data formatting | bytes 2097152

commit v2 on v1

--- a/solution.py
+++ b/solution.py
@@ -11,33 +11,31 @@
 MESH = pl.DeviceIdType.MESH
 
 
-def matrix_kernel(sources, rows_ref, cols_ref, count_ref, degree_ref, values_ref, out_ref, sums):
-    tile = values_ref.shape[1]
-    row_tiles = out_ref.shape[0] // tile
-
-    def clear(index, carry):
-        sums[index] = jnp.zeros(sums.shape[1:], jnp.float32)
-        return carry
-
-    lax.fori_loop(0, row_tiles * sources, clear, 0)
-
-    def add_slot(slot, carry):
+def order_kernel(sources, rows_ref, cols_ref, count_ref, before_ref, last_ref):
+    slots = rows_ref.shape[0]
+
+    def clear(place, carry):
+        last_ref[place] = slots
+        return carry
+
+    def skip(slot, carry):
+        before_ref[slot] = slots
+        return carry
+
+    def link(slot, carry):
         place = rows_ref[slot] * sources + cols_ref[slot]
-        sums[place] += values_ref[slot].astype(jnp.float32)
-        return carry
-
-    lax.fori_loop(0, count_ref[0], add_slot, 0)
-    for row in range(row_tiles):
-        degree = degree_ref[row : row + 1, :].astype(jnp.float32)
-        scale = (1.0 / jnp.broadcast_to(degree, (tile, tile))).T
-        for col in range(sources):
-            part = sums[row * sources + col] * scale
-            out_ref[row * tile : (row + 1) * tile, col * tile : (col + 1) * tile] = part.astype(jnp.bfloat16)
+        before_ref[slot] = last_ref[place]
+        last_ref[place] = slot
+        return carry
+
+    lax.fori_loop(0, last_ref.shape[0], clear, 0)
+    lax.fori_loop(0, slots, skip, 0)
+    lax.fori_loop(0, count_ref[0], link, 0)
 
 
 def step_kernel(
-    groups, ranks, send_ref, matrix_ref, block_ref, logs_ref, gram_ref,
-    source, own, staged, total, everyone, mine,
+    groups, ranks, send_ref, before_ref, last_ref, degree_ref, values_hbm, block_ref, logs_ref, gram_ref,
+    values_ref, sums, matrix_ref, values_sem, source, own, staged, total, everyone, mine,
     grp_send, grp_recv, row_send, row_recv, pass_send,
 ):
     chunks, _, row_tiles, tile, width = own.shape
@@ -47,6 +45,11 @@
     core = lax.rem(r, 2)
     partner = r + 1 - 2 * core
     pairs = ranks // 2
+
+    slots = values_ref.shape[0]
+    sources = source.shape[2]
+    load = pltpu.make_async_copy(values_hbm, values_ref, values_sem)
+    load.start()
 
     def other_group(step):
         return lax.rem(g + step, groups)
@@ -137,6 +140,23 @@
     pl.semaphore_wait(barrier, groups + ranks - 2)
     for j in range(chunks):
         send(0, j)
+    def clear(slot, carry):
+        sums[slot] = jnp.zeros(sums.shape[1:], jnp.float32)
+        return carry
+
+    def add_slot(slot, carry):
+        sums[slot] = sums[before_ref[slot]] + values_ref[slot].astype(jnp.float32)
+        return carry
+
+    lax.fori_loop(0, slots + 1, clear, 0)
+    load.wait()
+    lax.fori_loop(0, slots, add_slot, 0)
+    for row in range(row_tiles):
+        degree = degree_ref[row : row + 1, :].astype(jnp.float32)
+        scale = (1.0 / jnp.broadcast_to(degree, (tile, tile))).T
+        for col in range(sources):
+            part = sums[last_ref[row * sources + col]] * scale
+            matrix_ref[row * tile : (row + 1) * tile, col * tile : (col + 1) * tile] = part.astype(jnp.bfloat16)
     for phase in range(POWERS):
         for j in range(chunks):
             receive(phase, j)
@@ -183,14 +203,17 @@
     sources = ranks * row_tiles + groups
     smem = pl.BlockSpec(memory_space=pltpu.SMEM)
     vmem = pl.BlockSpec(memory_space=pltpu.VMEM)
-    matrix = pl.pallas_call(
-        functools.partial(matrix_kernel, sources),
-        out_shape=jax.ShapeDtypeStruct((rows_here, sources * tile), jnp.bfloat16),
-        in_specs=[smem, smem, smem, vmem, vmem],
-        out_specs=vmem,
-        scratch_shapes=[pltpu.VMEM((row_tiles * sources, tile, tile), jnp.float32)],
-        name="matrix",
-    )(tile_rows, tile_cols, tile_count, degree.reshape(row_tiles, tile), tile_values)
+    slots = tile_values.shape[0]
+    before, last = pl.pallas_call(
+        functools.partial(order_kernel, sources),
+        out_shape=(
+            jax.ShapeDtypeStruct((slots,), jnp.int32),
+            jax.ShapeDtypeStruct((row_tiles * sources,), jnp.int32),
+        ),
+        in_specs=[smem, smem, smem],
+        out_specs=(smem, smem),
+        name="order",
+    )(tile_rows, tile_cols, tile_count)
     share = width // ranks
     chunks = ranks
     dma = pltpu.SemaphoreType.DMA
@@ -200,9 +223,13 @@
             jax.ShapeDtypeStruct((rows_here, width), jnp.bfloat16),
             jax.ShapeDtypeStruct((share, width), jnp.float32),
         ),
-        in_specs=[smem, vmem, vmem],
+        in_specs=[smem, smem, smem, vmem, pl.BlockSpec(memory_space=pl.ANY), vmem],
         out_specs=(vmem, vmem),
         scratch_shapes=[
+            pltpu.VMEM(tile_values.shape, jnp.bfloat16),
+            pltpu.VMEM((slots + 1, tile, tile), jnp.float32),
+            pltpu.VMEM((rows_here, sources * tile), jnp.bfloat16),
+            dma,
             pltpu.VMEM((POWERS, chunks, sources, tile, share), jnp.bfloat16),
             pltpu.VMEM((chunks, POWERS + 1, row_tiles, tile, share), jnp.bfloat16),
             pltpu.VMEM((POWERS, chunks, groups, tile, share), jnp.bfloat16),
@@ -218,7 +245,7 @@
         compiler_params=pltpu.CompilerParams(
             collective_id=0, has_side_effects=True, vmem_limit_bytes=60 * 1024 * 1024),
         name="step",
-    )(send_tiles, matrix, block)
+    )(send_tiles, before, last, degree.reshape(row_tiles, tile), tile_values, block)
     return logs, gram
 
 

time: 117 us -> 116 us (level)
    pallas_call x1, Pallas kernels: 3.73 us -> 2.04 us  [body(): pl.pallas_call(functools.partial(order_kernel, sources), out_shape=(jax.S...]
where the time goes in v2:
time: 116 us; the launch traced here: 115 us
  Pallas kernels  110 us (95%)
  local copies, waits for them, and re-layouts  4.17 us (4%)
  between operations  1.29 us (1%)
    pallas_call x1, Pallas kernels, body(): pl.pallas_call(functools.partial(step_kernel, groups, ranks), out_shape=(...  108 us
    unnamed x2, local copies, waits for them, and re-layouts  4.17 us

profile of v2, /device:TPU:13, one launch (start us, length us, event | category | flops | bytes accessed | tf_op | source)
XLA Modules:
  0.0 115.4 jit_solution(8558491456419992944)
XLA Ops:
  1.3 2.0 %order.1 = (s32[64]{0:T(128)}, s32[32]{0:T(128)}) custom-call(s32[64]{0:T(128)} %rows_ref.1, s32[64]{0:T(128)} %cols_ref.1, s32[1]{0:T(128)S(6)} %copy.11.count_ref), custom_call_target="tpu_custom_call" | custom-call | tf_op jit(solution)/shard_map/order/pallas_call | solution.py:207
  3.3 107.8 %step.1 = (bf16[256,1024]{1,0:T(8,128)(2,1)}, f32[256,1024]{1,0:T(8,128)}) custom-call(s32[1,8]{1,0:T(1,128)} %send_ref.1, s32[64]{0:T(128)} %get-tuple-element.4.before_ref, s32[32]{0:T(128)} %get-tuple-element.5.last_ref, s32[2,128]{1,0:T(2,128)} %bitcast.1, bf16[64,128,128]{2,1,0:T(8,128)(2,1)} %values_hbm.1, bf16[256,1024]{1,0:T(8,128)(2,1)} %block_ref.1), custom_call_target="tpu_custom_call" | custom-call | tf_op jit(solution)/shard_map/step/pallas_call | solution.py:220
  111.2 1.9 %copy.12 = bf16[256,1024]{1,0:T(8,128)(2,1)} copy(bf16[256,1024]{1,0:T(8,128)(2,1)} %get-tuple-element.8) | data formatting | bytes 1048576
  113.1 2.3 %copy.13 = f32[256,1024]{1,0:T(8,128)} copy(f32[256,1024]{1,0:T(8,128)} %get-tuple-element.9) | data formatting | bytes 2097152

commit v3 on v2

--- a/solution.py
+++ b/solution.py
@@ -116,7 +116,7 @@
 
     def send(phase, j):
         if phase < POWERS:
-            for step in range(1, groups):
+            for step in sorted(range(1, groups), key=lambda step: abs(2 * step - groups)):
                 grp_copy(phase, j, other_group(step)).start()
         for step in range(1, pairs):
             row_copy(phase, j, same_core(step)).start()

time: 116 us -> 115 us (level)
  no operation moved by 1% of the time
where the time goes in v3:
time: 115 us
  Pallas kernels  110 us (96%)
  local copies, waits for them, and re-layouts  4.17 us (4%)
  between operations  1.29 us (1%)
    pallas_call x1, Pallas kernels, body(): pl.pallas_call(functools.partial(step_kernel, groups, ranks), out_shape=(...  107 us
    unnamed x2, local copies, waits for them, and re-layouts  4.17 us

profile of v3, /device:TPU:13, one launch (start us, length us, event | category | flops | bytes accessed | tf_op | source)
XLA Modules:
  0.0 115.1 jit_solution(12926513782095206072)
XLA Ops:
  1.3 2.3 %order.1 = (s32[64]{0:T(128)}, s32[32]{0:T(128)}) custom-call(s32[64]{0:T(128)} %rows_ref.1, s32[64]{0:T(128)} %cols_ref.1, s32[1]{0:T(128)S(6)} %copy.11.count_ref), custom_call_target="tpu_custom_call" | custom-call | tf_op jit(solution)/shard_map/order/pallas_call | solution.py:207
  3.6 107.4 %step.1 = (bf16[256,1024]{1,0:T(8,128)(2,1)}, f32[256,1024]{1,0:T(8,128)}) custom-call(s32[1,8]{1,0:T(1,128)} %send_ref.1, s32[64]{0:T(128)} %get-tuple-element.4.before_ref, s32[32]{0:T(128)} %get-tuple-element.5.last_ref, s32[2,128]{1,0:T(2,128)} %bitcast.1, bf16[64,128,128]{2,1,0:T(8,128)(2,1)} %values_hbm.1, bf16[256,1024]{1,0:T(8,128)(2,1)} %block_ref.1), custom_call_target="tpu_custom_call" | custom-call | tf_op jit(solution)/shard_map/step/pallas_call | solution.py:220
  110.9 1.9 %copy.12 = bf16[256,1024]{1,0:T(8,128)(2,1)} copy(bf16[256,1024]{1,0:T(8,128)(2,1)} %get-tuple-element.8) | data formatting | bytes 1048576
  112.8 2.3 %copy.13 = f32[256,1024]{1,0:T(8,128)} copy(f32[256,1024]{1,0:T(8,128)} %get-tuple-element.9) | data formatting | bytes 2097152
